TPU v7x, 32 devices: a whole 2x2x4 slice. The times are simulated.
32 devices in a mesh: pop: 2 (over x), chain: 16 (over z, y, core).
Axes of the slice: x: 2, y: 2, z: 4, core: 2. Of those that a mesh axis runs over, the one named last changes fastest.
Arguments:
- cost: float32 [8192, 4096], P(('pop', 'chain')), parts along dimension 0, may hold values from 0 to 20
- marginals: float32 [8192], P(('pop', 'chain')), parts along dimension 0, may hold values from 0.125 to 6
- final_marginal: float32 [8192], P('pop'), parts along dimension 0, may hold values from 0.125 to 6
Outputs:
- log_scaling: float32 [8192], P(('pop', 'chain')), parts along dimension 0
There are 2 independent parts, one for each index of `pop`. A program takes and returns all parts, laid end to end along the dimension named above; each array names one. Nothing has to cross between parts.
All inputs are finite; a program needn't handle non-finite values.
Results may differ from a plain program's by a relative error of at most 0.0001.
Values sent between devices are 32-bit elements; how exact they have to be, the bound alone decides.
No kernel may reach another device: no remote copies, remote signals or barrier semaphores. Data moves between devices by JAX's collectives and lax.ppermute only.
A program may use at most 64 MiB of HBM per device.

v0:
```python
import jax
import jax.numpy as jnp
from jax import lax
from jax.sharding import PartitionSpec as P

SWEEPS = 2


entropic = 0.25


def swapped(value, axis, apart):
    return lax.ppermute(value, axis, [(i, i ^ 1 << apart) for i in range(lax.axis_size(axis))])


def from_behind(block, axis, distance):
    devices = range(lax.axis_size(axis))
    route = [(i - distance, i) for i in devices if i - distance in devices]
    return lax.ppermute(block, axis, route)


def butterfly_sum(vector, width):
    for bit_index in range(width.bit_length() - 1):
        vector = vector + swapped(vector, "chain", bit_index)
    return vector


def doubling_gather(first, second, member, width):
    for bit_index in range(width.bit_length() - 1):
        other_first, other_second = swapped((first, second), "chain", bit_index)
        upward = member >> bit_index & 1 == 1
        first = jnp.where(
            upward, jnp.concatenate([other_first, first]), jnp.concatenate([first, other_first])
        )
        second = jnp.where(
            upward, jnp.concatenate([other_second, second]), jnp.concatenate([second, other_second])
        )
    return (first, second)


def on_device(cost, marginals, final_marginal):
    row_count = cost.shape[0]
    states = cost.shape[1]
    width = states // row_count
    kernels = lax.axis_size("chain") // width
    index = lax.axis_index("chain")
    group = index // width
    member = index % width
    kernel = jnp.exp(-cost / entropic)
    scaling = jnp.ones((row_count,), jnp.float32)
    last_scaling = jnp.ones((states,), jnp.float32)
    for sweep_index in range(SWEEPS):
        current = scaling
        alpha_start = jnp.ones((states,), jnp.float32)
        forward_state = (jnp.ones((row_count,), jnp.float32), current, alpha_start)
        backward_state = (jnp.ones((row_count,), jnp.float32), last_scaling)
        for position in range(kernels):
            partial_sums = jnp.dot(
                forward_state[1],
                kernel,
                precision=lax.Precision.HIGHEST,
                preferred_element_type=jnp.float32,
            )
            whole = butterfly_sum(partial_sums, width)
            forward_whole_alpha = whole * (states / jnp.sum(whole))
            forward_outgoing = lax.dynamic_slice_in_dim(
                forward_whole_alpha, member * row_count, row_count
            )
            forward_alpha_block, carried, forward_alpha_last = forward_state
            if position == kernels - 1:
                forward_alpha_last = forward_whole_alpha
            if position < kernels - 1:
                forward_arrived = from_behind(forward_outgoing, "chain", width)
                taking = group == position + 1
                forward_alpha_block = jnp.where(taking, forward_arrived, forward_alpha_block)
                carried = jnp.where(taking, current * forward_arrived, carried)
            forward_state = (forward_alpha_block, carried, forward_alpha_last)
        for position in range(kernels):
            backward_raw = jnp.dot(
                kernel,
                backward_state[1],
                precision=lax.Precision.HIGHEST,
                preferred_element_type=jnp.float32,
            )
            backward_raw_full, backward_weighted_full = doubling_gather(
                backward_raw, current * backward_raw, member, width
            )
            backward_beta_block, carried_full = backward_state
            target_step = kernels - 1 - position
            factor = states / jnp.sum(backward_raw_full)
            backward_beta_block = jnp.where(
                group == target_step, backward_raw * factor, backward_beta_block
            )
            if target_step > 0:
                arrived = from_behind(backward_weighted_full * factor, "chain", -width)
                carried_full = jnp.where(group == target_step - 1, arrived, carried_full)
            backward_state = (backward_beta_block, carried_full)
        alpha_block, carried_unused, alpha_last = forward_state
        beta_block = backward_state[0]
        scaling = marginals / (alpha_block * beta_block)
        last_scaling = final_marginal / alpha_last
    return jnp.log(scaling)


def solution(mesh):
    placed = (P(("pop", "chain"), None), P(("pop", "chain")), P("pop"))
    return jax.shard_map(
        on_device, mesh=mesh, in_specs=placed, out_specs=P(("pop", "chain")), check_vma=False
    )
```

profile of v0, /device:TPU:0, one launch (start us, length us, event | category | flops | bytes accessed | tf_op | source)
XLA Modules:
  0.0 41.0 jit_solution(11377174320524209963)
XLA Ops:
  0.0 0.0 copy-start
  0.0 0.0 copy-start.1
  0.0 4.6 %fusion.1 = f32[1,4096]{1,0:T(1,128)S(1)} fusion(f32[256,4096]{1,0:T(8,128)} %param.3), kind=kOutput, calls=%fused_computation.2 | convolution fusion | flops 14680064 | bytes 4210688 | tf_op jit(solution)/shard_map/dot_general | solution.py:58
  4.7 0.5 %collective-permute-start = (f32[4096]{0:T(1024)S(1)}, f32[4096]{0:T(1024)S(1)}, u32[]{:S(2)}, u32[]{:S(2)}) collective-permute-start(f32[4096]{0:T(1024)S(1)} %bitcast.4), channel_id=1, source_target_pairs={{0,1},{1,0},{2,3},{3,2},{4,5},{5,4},{6,7},{7,6},{8,9},{9,8},{10,11... | collective-permute-start | bytes 49160 | tf_op jit(solution)/shard_map/ppermute | solution.py:13
  5.2 0.8 %collective-permute-done = f32[4096]{0:T(1024)S(1)} collective-permute-done((f32[4096]{0:T(1024)S(1)}, f32[4096]{0:T(1024)S(1)}, u32[]{:S(2)}, u32[]{:S(2)}) %collective-permute-start) | collective-permute-done | bytes 16416 | tf_op jit(solution)/shard_map/ppermute | solution.py:13
  6.0 2.8 %collective-permute-start.1 = (f32[4096]{0:T(1024)S(1)}, f32[4096]{0:T(1024)S(1)}, u32[]{:S(2)}, u32[]{:S(2)}) collective-permute-start(f32[4096]{0:T(1024)S(1)} %add.17), channel_id=1, source_target_pairs={{0,2},{1,3},{2,0},{3,1},{4,6},{5,7},{6,4},{7,5},{8,10},{9,11},{10,... | collective-permute-start | bytes 49160 | tf_op jit(solution)/shard_map/ppermute | solution.py:13
  8.8 1.7 %collective-permute-done.1 = f32[4096]{0:T(1024)S(1)} collective-permute-done((f32[4096]{0:T(1024)S(1)}, f32[4096]{0:T(1024)S(1)}, u32[]{:S(2)}, u32[]{:S(2)}) %collective-permute-start.1) | collective-permute-done | bytes 16416 | tf_op jit(solution)/shard_map/ppermute | solution.py:13
  10.6 2.1 %collective-permute-start.2 = (f32[4096]{0:T(1024)S(1)}, f32[4096]{0:T(1024)S(1)}, u32[]{:S(2)}, u32[]{:S(2)}) collective-permute-start(f32[4096]{0:T(1024)S(1)} %add.18), channel_id=1, source_target_pairs={{0,4},{1,5},{2,6},{3,7},{4,0},{5,1},{6,2},{7,3},{8,12},{9,13},{10,... | collective-permute-start | bytes 49160 | tf_op jit(solution)/shard_map/ppermute | solution.py:13
  12.7 1.7 %collective-permute-done.2 = f32[4096]{0:T(1024)S(1)} collective-permute-done((f32[4096]{0:T(1024)S(1)}, f32[4096]{0:T(1024)S(1)}, u32[]{:S(2)}, u32[]{:S(2)}) %collective-permute-start.2) | collective-permute-done | bytes 16416 | tf_op jit(solution)/shard_map/ppermute | solution.py:13
  14.4 3.0 %collective-permute-start.3 = (f32[4096]{0:T(1024)S(1)}, f32[4096]{0:T(1024)S(1)}, u32[]{:S(2)}, u32[]{:S(2)}) collective-permute-start(f32[4096]{0:T(1024)S(1)} %add.19), channel_id=1, source_target_pairs={{0,8},{1,9},{2,10},{3,11},{4,12},{5,13},{6,14},{7,15},{8,0},{9,1},... | collective-permute-start | bytes 49160 | tf_op jit(solution)/shard_map/ppermute | solution.py:13
  17.4 1.7 %collective-permute-done.3 = f32[4096]{0:T(1024)S(1)} collective-permute-done((f32[4096]{0:T(1024)S(1)}, f32[4096]{0:T(1024)S(1)}, u32[]{:S(2)}, u32[]{:S(2)}) %collective-permute-start.3) | collective-permute-done | bytes 16416 | tf_op jit(solution)/shard_map/ppermute | solution.py:13
  19.1 0.6 %fusion.10 = (f32[]{:T(128)}, f32[4096]{0:T(1024)S(1)}) fusion(f32[4096]{0:T(1024)S(1)} %add.19, f32[4096]{0:T(1024)S(1)} %collective-permute-done.3), kind=kLoop, calls=%fused_computation.17 | loop fusion | flops 8191 | bytes 49156 | tf_op jit(solution)/shard_map/reduce_sum | solution.py:65
  20.4 0.0 copy-done
  20.4 5.7 %fusion = f32[1,256]{1,0:T(1,128)S(1)} fusion(f32[4096,1]{0,1:T(1,128)S(1)} %bitcast.6, f32[256,4096]{1,0:T(8,128)} %param.3), kind=kOutput, calls=%fused_computation.1 | convolution fusion | flops 14680064 | bytes 4211712 | tf_op jit(solution)/shard_map/dot_general | solution.py:79
  26.1 0.0 collective-permute-start.4
  26.2 1.2 %collective-permute-done.4 = f32[256]{0:T(256)S(1)} collective-permute-done((f32[256]{0:T(256)S(1)}, f32[256]{0:T(256)S(1)}, u32[]{:S(2)}, u32[]{:S(2)}) %collective-permute-start.4) | collective-permute-done | bytes 1056 | tf_op jit(solution)/shard_map/ppermute | solution.py:13
  27.3 1.9 %collective-permute-start.5 = (f32[512]{0:T(512)S(1)}, f32[512]{0:T(512)S(1)}, u32[]{:S(2)}, u32[]{:S(2)}) collective-permute-start(f32[512]{0:T(512)S(1)} %maximum_select_fusion.3), channel_id=1, source_target_pairs={{0,2},{1,3},{2,0},{3,1},{4,6},{5,7},{6,4},{7,5},{8,10},{9,11},{10,... | collective-permute-start | bytes 6152 | tf_op jit(solution)/shard_map/ppermute | solution.py:13
  29.2 1.7 %collective-permute-done.5 = f32[512]{0:T(512)S(1)} collective-permute-done((f32[512]{0:T(512)S(1)}, f32[512]{0:T(512)S(1)}, u32[]{:S(2)}, u32[]{:S(2)}) %collective-permute-start.5) | collective-permute-done | bytes 2080 | tf_op jit(solution)/shard_map/ppermute | solution.py:13
  30.9 1.9 %collective-permute-start.6 = (f32[1024]{0:T(1024)S(1)}, f32[1024]{0:T(1024)S(1)}, u32[]{:S(2)}, u32[]{:S(2)}) collective-permute-start(f32[1024]{0:T(1024)S(1)} %maximum_select_fusion.2), channel_id=1, source_target_pairs={{0,4},{1,5},{2,6},{3,7},{4,0},{5,1},{6,2},{7,3},{8,12},{9,13},{10,... | collective-permute-start | bytes 12296 | tf_op jit(solution)/shard_map/ppermute | solution.py:13
  32.8 1.7 %collective-permute-done.6 = f32[1024]{0:T(1024)S(1)} collective-permute-done((f32[1024]{0:T(1024)S(1)}, f32[1024]{0:T(1024)S(1)}, u32[]{:S(2)}, u32[]{:S(2)}) %collective-permute-start.6) | collective-permute-done | bytes 4128 | tf_op jit(solution)/shard_map/ppermute | solution.py:13
  34.5 2.9 %collective-permute-start.7 = (f32[2048]{0:T(1024)S(1)}, f32[2048]{0:T(1024)S(1)}, u32[]{:S(2)}, u32[]{:S(2)}) collective-permute-start(f32[2048]{0:T(1024)S(1)} %maximum_select_fusion.1), channel_id=1, source_target_pairs={{0,8},{1,9},{2,10},{3,11},{4,12},{5,13},{6,14},{7,15},{8,0},{9,1},... | collective-permute-start | bytes 24584 | tf_op jit(solution)/shard_map/ppermute | solution.py:13
  37.5 1.6 %collective-permute-done.7 = f32[2048]{0:T(1024)S(1)} collective-permute-done((f32[2048]{0:T(1024)S(1)}, f32[2048]{0:T(1024)S(1)}, u32[]{:S(2)}, u32[]{:S(2)}) %collective-permute-start.7) | collective-permute-done | bytes 8224 | tf_op jit(solution)/shard_map/ppermute | solution.py:13
  39.1 0.6 %fusion.4 = f32[]{:T(128)} fusion(f32[2048]{0:T(1024)S(1)} %maximum_select_fusion.1, f32[2048]{0:T(1024)S(1)} %collective-permute-done.7, pred[]{:T(512)S(6)} %eq.18), kind=kLoop, calls=%fused_computation.6 | loop fusion | flops 16383 | bytes 16389 | tf_op jit(solution)/shard_map/reduce_sum | solution.py:90
  40.4 0.0 copy-done.1
  40.4 0.6 %fusion.5 = f32[256]{0:T(256)} fusion(f32[256]{0:T(256)S(1)} %copy-done.1, f32[256]{0:T(256)S(1)} %bitcast.9, pred[]{:T(512)S(6)} %eq.17, f32[]{:T(128)S(6)} %div.33), kind=kLoop, calls=%fused_computation.12 | loop fusion | flops 768 | bytes 3077 | tf_op jit(solution)/shard_map/log | solution.py:102
  (7 shorter events, 0.0 us)
Async XLA Ops:
  0.0 20.4 %copy-start = (f32[4096]{0:T(1024)S(1)}, f32[4096]{0:T(1024)}, u32[]{:S(2)}) copy-start(f32[4096]{0:T(1024)} %param.5) | copy-start | bytes 49156
  0.0 40.4 %copy-start.1 = (f32[256]{0:T(256)S(1)}, f32[256]{0:T(256)}, u32[]{:S(2)}) copy-start(f32[256]{0:T(256)} %param.4) | copy-start | bytes 3076
  4.7 1.3 %collective-permute-start = (f32[4096]{0:T(1024)S(1)}, f32[4096]{0:T(1024)S(1)}, u32[]{:S(2)}, u32[]{:S(2)}) collective-permute-start(f32[4096]{0:T(1024)S(1)} %bitcast.4), channel_id=1, source_target_pairs={{0,1},{1,0},{2,3},{3,2},{4,5},{5,4},{6,7},{7,6},{8,9},{9,8},{10,11... | collective-permute-start | bytes 49160 | tf_op jit(solution)/shard_map/ppermute | solution.py:13
  6.0 4.6 %collective-permute-start.1 = (f32[4096]{0:T(1024)S(1)}, f32[4096]{0:T(1024)S(1)}, u32[]{:S(2)}, u32[]{:S(2)}) collective-permute-start(f32[4096]{0:T(1024)S(1)} %add.17), channel_id=1, source_target_pairs={{0,2},{1,3},{2,0},{3,1},{4,6},{5,7},{6,4},{7,5},{8,10},{9,11},{10,... | collective-permute-start | bytes 49160 | tf_op jit(solution)/shard_map/ppermute | solution.py:13
  10.6 3.8 %collective-permute-start.2 = (f32[4096]{0:T(1024)S(1)}, f32[4096]{0:T(1024)S(1)}, u32[]{:S(2)}, u32[]{:S(2)}) collective-permute-start(f32[4096]{0:T(1024)S(1)} %add.18), channel_id=1, source_target_pairs={{0,4},{1,5},{2,6},{3,7},{4,0},{5,1},{6,2},{7,3},{8,12},{9,13},{10,... | collective-permute-start | bytes 49160 | tf_op jit(solution)/shard_map/ppermute | solution.py:13
  14.4 4.8 %collective-permute-start.3 = (f32[4096]{0:T(1024)S(1)}, f32[4096]{0:T(1024)S(1)}, u32[]{:S(2)}, u32[]{:S(2)}) collective-permute-start(f32[4096]{0:T(1024)S(1)} %add.19), channel_id=1, source_target_pairs={{0,8},{1,9},{2,10},{3,11},{4,12},{5,13},{6,14},{7,15},{8,0},{9,1},... | collective-permute-start | bytes 49160 | tf_op jit(solution)/shard_map/ppermute | solution.py:13
  26.1 1.2 %collective-permute-start.4 = (f32[256]{0:T(256)S(1)}, f32[256]{0:T(256)S(1)}, u32[]{:S(2)}, u32[]{:S(2)}) collective-permute-start(f32[256]{0:T(256)S(1)} %bitcast.7), channel_id=1, source_target_pairs={{0,1},{1,0},{2,3},{3,2},{4,5},{5,4},{6,7},{7,6},{8,9},{9,8},{10,11... | collective-permute-start | bytes 3080 | tf_op jit(solution)/shard_map/ppermute | solution.py:13
  27.3 3.6 %collective-permute-start.5 = (f32[512]{0:T(512)S(1)}, f32[512]{0:T(512)S(1)}, u32[]{:S(2)}, u32[]{:S(2)}) collective-permute-start(f32[512]{0:T(512)S(1)} %maximum_select_fusion.3), channel_id=1, source_target_pairs={{0,2},{1,3},{2,0},{3,1},{4,6},{5,7},{6,4},{7,5},{8,10},{9,11},{10,... | collective-permute-start | bytes 6152 | tf_op jit(solution)/shard_map/ppermute | solution.py:13
  30.9 3.6 %collective-permute-start.6 = (f32[1024]{0:T(1024)S(1)}, f32[1024]{0:T(1024)S(1)}, u32[]{:S(2)}, u32[]{:S(2)}) collective-permute-start(f32[1024]{0:T(1024)S(1)} %maximum_select_fusion.2), channel_id=1, source_target_pairs={{0,4},{1,5},{2,6},{3,7},{4,0},{5,1},{6,2},{7,3},{8,12},{9,13},{10,... | collective-permute-start | bytes 12296 | tf_op jit(solution)/shard_map/ppermute | solution.py:13
  34.5 4.6 %collective-permute-start.7 = (f32[2048]{0:T(1024)S(1)}, f32[2048]{0:T(1024)S(1)}, u32[]{:S(2)}, u32[]{:S(2)}) collective-permute-start(f32[2048]{0:T(1024)S(1)} %maximum_select_fusion.1), channel_id=1, source_target_pairs={{0,8},{1,9},{2,10},{3,11},{4,12},{5,13},{6,14},{7,15},{8,0},{9,1},... | collective-permute-start | bytes 24584 | tf_op jit(solution)/shard_map/ppermute | solution.py:13
where the time goes:
time: 41.2 us; the launch traced here: 41 us
  starting transfers between devices  15.2 us (37%)
  waiting for transfers between devices  12.2 us (30%)
  matrix products  10.3 us (25%)
  other arithmetic  1.83 us (4%)
  between operations  1.44 us (3%)
    ppermute x8, starting transfers between devices, swapped(): lax.ppermute(value, axis, [(i, i ^ 1 << apart) for i in range(lax.axis_si...  15.2 us
    ppermute x8, waiting for transfers between devices, swapped(): lax.ppermute(value, axis, [(i, i ^ 1 << apart) for i in range(lax.axis_si...  12.2 us
    dot_general x1, matrix products, on_device(): jnp.dot(kernel, backward_state[1], precision=lax.Precision.HIGHEST, prefe...  5.7 us
    dot_general x1, matrix products, on_device(): jnp.dot(forward_state[1], kernel, precision=lax.Precision.HIGHEST, prefer...  4.65 us
  transfers between devices with their start and end apart: 8, of which 8 were waited for; matrix products, arithmetic and copies ran while one was open for 0% of the time, Pallas kernels for 0%

commit v1 on v0

--- a/solution.py
+++ b/solution.py
@@ -1,16 +1,121 @@
 import jax
 import jax.numpy as jnp
 from jax import lax
+from jax.experimental import pallas as pl
+from jax.experimental.pallas import tpu as pltpu
 from jax.sharding import PartitionSpec as P
 
 SWEEPS = 2
+LANES = 128
+SUBLANES = 8
+CHUNKS = 8
 
 
 entropic = 0.25
+EXP2_SCALE = -1.4426950408889634 / entropic
 
 
 def swapped(value, axis, apart):
-    return lax.ppermute(value, axis, [(i, i ^ 1 << apart) for i in range(lax.axis_size(axis))])
+    return lax.ppermute(value, axis, [(i, i ^ apart) for i in range(lax.axis_size(axis))])
+
+
+def distances(width):
+    return [1 << bit_index | 1 for bit_index in range(width.bit_length() - 1)]
+
+
+def butterfly_sum(vector, width):
+    for apart in distances(width):
+        vector = vector + swapped(vector, "chain", apart)
+    return vector
+
+
+def kernel_and_sums(cost):
+    rows, states = cost.shape
+    tiles = states // LANES
+    chunk = rows // CHUNKS
+
+    def body(cost_ref, kernel_ref, sums_ref, sems):
+        def copy(index):
+            span = pl.ds(index * chunk, chunk)
+            return pltpu.make_async_copy(cost_ref.at[span], kernel_ref.at[span], sems.at[index])
+
+        for index in range(CHUNKS):
+            copy(index).start()
+        totals = [jnp.zeros((SUBLANES, LANES), jnp.float32)] * tiles
+        for index in range(CHUNKS):
+            copy(index).wait()
+            for first in range(index * chunk, (index + 1) * chunk, SUBLANES):
+                for tile in range(tiles):
+                    at = (pl.ds(first, SUBLANES), pl.ds(tile * LANES, LANES))
+                    value = jnp.exp2(kernel_ref[at] * EXP2_SCALE)
+                    kernel_ref[at] = value
+                    totals[tile] = totals[tile] + value
+        for tile in range(tiles):
+            sums_ref[pl.ds(tile, 1), :] = jnp.sum(totals[tile], axis=0, keepdims=True)
+
+    return pl.pallas_call(
+        body,
+        out_shape=(
+            jax.ShapeDtypeStruct((rows, states), jnp.float32),
+            jax.ShapeDtypeStruct((tiles, LANES), jnp.float32),
+        ),
+        in_specs=[pl.BlockSpec(memory_space=pltpu.HBM)],
+        out_specs=[pl.BlockSpec(memory_space=pltpu.VMEM)] * 2,
+        scratch_shapes=[pltpu.SemaphoreType.DMA((CHUNKS,))],
+        compiler_params=pltpu.CompilerParams(vmem_limit_bytes=16 << 20),
+        name="kernel_and_sums",
+    )(cost)
+
+
+def log_row_scaling(kernel, half, other_half, final_marginal, marginals):
+    rows, states = kernel.shape
+    tiles = states // LANES
+
+    def body(kernel_ref, half_ref, other_ref, final_ref, marginal_ref, out_ref, weight_ref):
+        final = final_ref[...]
+        weight_ref[...] = final * float(states) / (half_ref[...] + other_ref[...])
+        total = jnp.sum(final, keepdims=True)
+        weights = [
+            jnp.broadcast_to(weight_ref[pl.ds(tile, 1), :], (SUBLANES, LANES)) for tile in range(tiles)
+        ]
+        partial = []
+        for first in range(0, rows, SUBLANES):
+            sums = [None] * 4
+            for tile in range(tiles):
+                at = (pl.ds(first, SUBLANES), pl.ds(tile * LANES, LANES))
+                term = kernel_ref[at] * weights[tile]
+                sums[tile % 4] = term if sums[tile % 4] is None else sums[tile % 4] + term
+            partial.append((sums[0] + sums[1]) + (sums[2] + sums[3]))
+        for block in range(rows // LANES):
+            square = jnp.concatenate(partial[block * 16 : block * 16 + 16], axis=0)
+            row_sums = jnp.sum(square.T, axis=0, keepdims=True)
+            at = (pl.ds(block, 1), slice(None))
+            out_ref[at] = jnp.log(marginal_ref[at] * total / row_sums)
+
+    return pl.pallas_call(
+        body,
+        out_shape=jax.ShapeDtypeStruct((rows // LANES, LANES), jnp.float32),
+        in_specs=[pl.BlockSpec(memory_space=pltpu.VMEM)] * 5,
+        out_specs=pl.BlockSpec(memory_space=pltpu.VMEM),
+        scratch_shapes=[pltpu.VMEM((tiles, LANES), jnp.float32)],
+        compiler_params=pltpu.CompilerParams(vmem_limit_bytes=16 << 20),
+        name="log_row_scaling",
+    )(
+        kernel,
+        half,
+        other_half,
+        final_marginal.reshape(tiles, LANES),
+        marginals.reshape(rows // LANES, LANES),
+    ).reshape(rows)
+
+
+def one_kernel(cost, marginals, final_marginal):
+    width = cost.shape[1] // cost.shape[0]
+    kernel, sums = kernel_and_sums(cost)
+    *early, last = distances(width)
+    for apart in early:
+        sums = sums + swapped(sums, "chain", apart)
+    return log_row_scaling(kernel, sums, swapped(sums, "chain", last), final_marginal, marginals)
 
 
 def from_behind(block, axis, distance):
@@ -19,15 +124,9 @@
     return lax.ppermute(block, axis, route)
 
 
-def butterfly_sum(vector, width):
-    for bit_index in range(width.bit_length() - 1):
-        vector = vector + swapped(vector, "chain", bit_index)
-    return vector
-
-
 def doubling_gather(first, second, member, width):
     for bit_index in range(width.bit_length() - 1):
-        other_first, other_second = swapped((first, second), "chain", bit_index)
+        other_first, other_second = (swapped(part, "chain", 1 << bit_index) for part in (first, second))
         upward = member >> bit_index & 1 == 1
         first = jnp.where(
             upward, jnp.concatenate([other_first, first]), jnp.concatenate([first, other_first])
@@ -38,7 +137,7 @@
     return (first, second)
 
 
-def on_device(cost, marginals, final_marginal):
+def many_kernels(cost, marginals, final_marginal):
     row_count = cost.shape[0]
     states = cost.shape[1]
     width = states // row_count
@@ -102,6 +201,13 @@
     return jnp.log(scaling)
 
 
+def on_device(cost, marginals, final_marginal):
+    width = cost.shape[1] // cost.shape[0]
+    if lax.axis_size("chain") == width:
+        return one_kernel(cost, marginals, final_marginal)
+    return many_kernels(cost, marginals, final_marginal)
+
+
 def solution(mesh):
     placed = (P(("pop", "chain"), None), P(("pop", "chain")), P("pop"))
     return jax.shard_map(

time: 41.2 us -> 17.2 us (0.42)
  matrix products: 10.3 us -> 0 us
  starting transfers between devices: 15.2 us -> 7.68 us
  waiting for transfers between devices: 12.2 us -> 5.17 us
  local copies, waits for them, and re-layouts: 0.01 us -> 2.19 us
  Pallas kernels: 0 us -> 1.95 us
  other arithmetic: 1.83 us -> 0.01 us
  between operations: 1.44 us -> 0.02 us
    dot_general x2 -> x0, matrix products: 10.3 us -> none  [the longest x1 5.7 us: on_device(): jnp.dot(kernel, backward_state[1], precision=lax.Precision.HIGHEST, prefe...]
    ppermute x8 -> x4, starting transfers between devices: 15.2 us -> 7.68 us  [swapped(): lax.ppermute(value, axis, [(i, i ^ apart) for i in range(lax.axis_size(ax...]
    ppermute x8 -> x4, waiting for transfers between devices: 12.2 us -> 5.17 us  [swapped(): lax.ppermute(value, axis, [(i, i ^ apart) for i in range(lax.axis_size(ax...]
    unnamed x4 -> x6, local copies, waits for them, and re-layouts: 0.01 us -> 2.19 us
    pallas_call x0 -> x2, Pallas kernels: none -> 1.95 us  [the longest x1 0.99 us: kernel_and_sums(): pl.pallas_call(body, out_shape=(jax.ShapeDtypeStruct((rows, states), jnp....]
    reduce_sum x2 -> x0, other arithmetic: 1.2 us -> none  [the longest x1 0.6 us: on_device(): factor = states / jnp.sum(backward_raw_full)]
    log x1 -> x0, other arithmetic: 0.58 us -> none  [on_device(): return jnp.log(scaling)]
  transfers between devices with their start and end apart: 8 -> 4, of which waited for: 8 -> 4; matrix products, arithmetic and copies ran while one was open for 0% -> 0% of each run, Pallas kernels for 0% -> 0%
where the time goes in v1:
time: 17.2 us; the launch traced here: 17 us
  starting transfers between devices  7.68 us (45%)
  waiting for transfers between devices  5.17 us (30%)
  local copies, waits for them, and re-layouts  2.19 us (13%)
  Pallas kernels  1.95 us (11%)
    ppermute x4, starting transfers between devices, swapped(): lax.ppermute(value, axis, [(i, i ^ apart) for i in range(lax.axis_size(ax...  7.68 us
    ppermute x4, waiting for transfers between devices, swapped(): lax.ppermute(value, axis, [(i, i ^ apart) for i in range(lax.axis_size(ax...  5.17 us
    unnamed x6, local copies, waits for them, and re-layouts  2.19 us
    pallas_call x1, Pallas kernels, kernel_and_sums(): pl.pallas_call(body, out_shape=(jax.ShapeDtypeStruct((rows, states), jnp....  0.99 us
    pallas_call x1, Pallas kernels, log_row_scaling(): pl.pallas_call(body, out_shape=jax.ShapeDtypeStruct((rows // LANES, LANES...  0.96 us
  transfers between devices with their start and end apart: 4, of which 4 were waited for; matrix products, arithmetic and copies ran while one was open for 0% of the time, Pallas kernels for 0%

profile of v1, /device:TPU:0, one launch (start us, length us, event | category | flops | bytes accessed | tf_op | source)
XLA Modules:
  0.0 17.0 jit_solution(16132406245199265885)
XLA Ops:
  0.0 0.0 copy-start
  0.0 2.2 %copy-done = f32[256,4096]{1,0:T(8,128)S(1)} copy-done((f32[256,4096]{1,0:T(8,128)S(1)}, f32[256,4096]{1,0:T(8,128)}, u32[]{:S(2)}) %copy-start) | copy-done | bytes 4194328
  2.2 0.0 copy-start.1
  2.2 0.0 copy-start.2
  2.2 1.0 %kernel_and_sums.1 = (f32[256,4096]{1,0:T(8,128)S(1)}, f32[32,128]{1,0:T(8,128)S(1)}) custom-call(f32[256,4096]{1,0:T(8,128)S(1)} %copy-done), custom_call_target="tpu_custom_call" | custom-call | tf_op jit(solution)/shard_map/kernel_and_sums/pallas_call | solution.py:56
  3.2 0.6 %collective-permute-start = (f32[32,128]{1,0:T(8,128)S(1)}, f32[32,128]{1,0:T(8,128)S(1)}, u32[]{:S(2)}, u32[]{:S(2)}) collective-permute-start(f32[32,128]{1,0:T(8,128)S(1)} %get-tuple-element.8), channel_id=1, source_target_pairs={{0,1},{1,0},{2,3},{3,2},{4,5},{5,4},{6,7},{7,6},{8,9},{9,8},{10,11... | collective-permute-start | bytes 49160 | tf_op jit(solution)/shard_map/ppermute | solution.py:19
  3.8 0.8 %collective-permute-done = f32[32,128]{1,0:T(8,128)S(1)} collective-permute-done((f32[32,128]{1,0:T(8,128)S(1)}, f32[32,128]{1,0:T(8,128)S(1)}, u32[]{:S(2)}, u32[]{:S(2)}) %collective-permute-start) | collective-permute-done | bytes 16416 | tf_op jit(solution)/shard_map/ppermute | solution.py:19
  4.6 2.6 %collective-permute-start.1 = (f32[32,128]{1,0:T(8,128)S(1)}, f32[32,128]{1,0:T(8,128)S(1)}, u32[]{:S(2)}, u32[]{:S(2)}) collective-permute-start(f32[32,128]{1,0:T(8,128)S(1)} %add.9), channel_id=1, source_target_pairs={{0,3},{1,2},{2,1},{3,0},{4,7},{5,6},{6,5},{7,4},{8,11},{9,10},{10,... | collective-permute-start | bytes 49160 | tf_op jit(solution)/shard_map/ppermute | solution.py:19
  7.2 1.4 %collective-permute-done.1 = f32[32,128]{1,0:T(8,128)S(1)} collective-permute-done((f32[32,128]{1,0:T(8,128)S(1)}, f32[32,128]{1,0:T(8,128)S(1)}, u32[]{:S(2)}, u32[]{:S(2)}) %collective-permute-start.1) | collective-permute-done | bytes 16416 | tf_op jit(solution)/shard_map/ppermute | solution.py:19
  8.7 1.8 %collective-permute-start.2 = (f32[32,128]{1,0:T(8,128)S(1)}, f32[32,128]{1,0:T(8,128)S(1)}, u32[]{:S(2)}, u32[]{:S(2)}) collective-permute-start(f32[32,128]{1,0:T(8,128)S(1)} %add.10), channel_id=1, source_target_pairs={{0,5},{1,4},{2,7},{3,6},{4,1},{5,0},{6,3},{7,2},{8,13},{9,12},{10,... | collective-permute-start | bytes 49160 | tf_op jit(solution)/shard_map/ppermute | solution.py:19
  10.4 1.4 %collective-permute-done.2 = f32[32,128]{1,0:T(8,128)S(1)} collective-permute-done((f32[32,128]{1,0:T(8,128)S(1)}, f32[32,128]{1,0:T(8,128)S(1)}, u32[]{:S(2)}, u32[]{:S(2)}) %collective-permute-start.2) | collective-permute-done | bytes 16416 | tf_op jit(solution)/shard_map/ppermute | solution.py:19
  11.9 2.7 %collective-permute-start.3 = (f32[32,128]{1,0:T(8,128)S(1)}, f32[32,128]{1,0:T(8,128)S(1)}, u32[]{:S(2)}, u32[]{:S(2)}) collective-permute-start(f32[32,128]{1,0:T(8,128)S(1)} %add.11.half_ref), channel_id=1, source_target_pairs={{0,9},{1,8},{2,11},{3,10},{4,13},{5,12},{6,15},{7,14},{8,1},{9,0},... | collective-permute-start | bytes 49160 | tf_op jit(solution)/shard_map/ppermute | solution.py:19
  14.6 1.4 %collective-permute-done.3.other_ref = f32[32,128]{1,0:T(8,128)S(1)} collective-permute-done((f32[32,128]{1,0:T(8,128)S(1)}, f32[32,128]{1,0:T(8,128)S(1)}, u32[]{:S(2)}, u32[]{:S(2)}) %collective-permute-start.3) | collective-permute-done | bytes 16416 | tf_op jit(solution)/shard_map/ppermute | solution.py:19
  16.1 0.0 copy-done.1
  16.1 0.0 copy-done.2
  16.1 1.0 %log_row_scaling.1 = f32[2,128]{1,0:T(2,128)} custom-call(f32[256,4096]{1,0:T(8,128)S(1)} %get-tuple-element.7.kernel_ref, f32[32,128]{1,0:T(8,128)S(1)} %add.11.half_ref, f32[32,128]{1,0:T(8,128)S(1)} %collective-permute-done.3.other_ref, f32[32,128]{1,0:T(8,128)S(1)} %bitcast.3, f32[2,128]{1,0:T(2,128)S(1)} %bitcast.4), custom_call_target="tpu_custom_call" | custom-call | tf_op jit(solution)/shard_map/log_row_scaling/pallas_call | solution.py:95
  (3 shorter events, 0.0 us)
Async XLA Ops:
  0.0 2.2 %copy-start = (f32[256,4096]{1,0:T(8,128)S(1)}, f32[256,4096]{1,0:T(8,128)}, u32[]{:S(2)}) copy-start(f32[256,4096]{1,0:T(8,128)} %cost_ref.1) | copy-start | bytes 12582916
  2.2 13.9 %copy-start.1 = (f32[4096]{0:T(1024)S(1)}, f32[4096]{0:T(1024)}, u32[]{:S(2)}) copy-start(f32[4096]{0:T(1024)} %param.5) | copy-start | bytes 49156
  2.2 13.9 %copy-start.2 = (f32[256]{0:T(256)S(1)}, f32[256]{0:T(256)}, u32[]{:S(2)}) copy-start(f32[256]{0:T(256)} %param.4) | copy-start | bytes 3076
  3.2 1.4 %collective-permute-start = (f32[32,128]{1,0:T(8,128)S(1)}, f32[32,128]{1,0:T(8,128)S(1)}, u32[]{:S(2)}, u32[]{:S(2)}) collective-permute-start(f32[32,128]{1,0:T(8,128)S(1)} %get-tuple-element.8), channel_id=1, source_target_pairs={{0,1},{1,0},{2,3},{3,2},{4,5},{5,4},{6,7},{7,6},{8,9},{9,8},{10,11... | collective-permute-start | bytes 49160 | tf_op jit(solution)/shard_map/ppermute | solution.py:19
  4.6 4.1 %collective-permute-start.1 = (f32[32,128]{1,0:T(8,128)S(1)}, f32[32,128]{1,0:T(8,128)S(1)}, u32[]{:S(2)}, u32[]{:S(2)}) collective-permute-start(f32[32,128]{1,0:T(8,128)S(1)} %add.9), channel_id=1, source_target_pairs={{0,3},{1,2},{2,1},{3,0},{4,7},{5,6},{6,5},{7,4},{8,11},{9,10},{10,... | collective-permute-start | bytes 49160 | tf_op jit(solution)/shard_map/ppermute | solution.py:19
  8.7 3.2 %collective-permute-start.2 = (f32[32,128]{1,0:T(8,128)S(1)}, f32[32,128]{1,0:T(8,128)S(1)}, u32[]{:S(2)}, u32[]{:S(2)}) collective-permute-start(f32[32,128]{1,0:T(8,128)S(1)} %add.10), channel_id=1, source_target_pairs={{0,5},{1,4},{2,7},{3,6},{4,1},{5,0},{6,3},{7,2},{8,13},{9,12},{10,... | collective-permute-start | bytes 49160 | tf_op jit(solution)/shard_map/ppermute | solution.py:19
  11.9 4.2 %collective-permute-start.3 = (f32[32,128]{1,0:T(8,128)S(1)}, f32[32,128]{1,0:T(8,128)S(1)}, u32[]{:S(2)}, u32[]{:S(2)}) collective-permute-start(f32[32,128]{1,0:T(8,128)S(1)} %add.11.half_ref), channel_id=1, source_target_pairs={{0,9},{1,8},{2,11},{3,10},{4,13},{5,12},{6,15},{7,14},{8,1},{9,0},... | collective-permute-start | bytes 49160 | tf_op jit(solution)/shard_map/ppermute | solution.py:19

commit v2 on v1

--- a/solution.py
+++ b/solution.py
@@ -64,7 +64,7 @@
         scratch_shapes=[pltpu.SemaphoreType.DMA((CHUNKS,))],
         compiler_params=pltpu.CompilerParams(vmem_limit_bytes=16 << 20),
         name="kernel_and_sums",
-    )(cost)
+    )(pltpu.with_memory_space_constraint(cost, pltpu.HBM))
 
 
 def log_row_scaling(kernel, half, other_half, final_marginal, marginals):

time: 17.2 us -> 16.3 us (0.948)
  local copies, waits for them, and re-layouts: 2.19 us -> 0.01 us
  Pallas kernels: 1.95 us -> 3.29 us
    unnamed x6 -> x4, local copies, waits for them, and re-layouts: 2.19 us -> 0.01 us
    pallas_call x1, Pallas kernels: 0.99 us -> 2.34 us  [kernel_and_sums(): pl.pallas_call(body, out_shape=(jax.ShapeDtypeStruct((rows, states), jnp....]
where the time goes in v2:
time: 16.3 us; the launch traced here: 16.2 us
  starting transfers between devices  7.68 us (47%)
  waiting for transfers between devices  5.17 us (32%)
  Pallas kernels  3.29 us (20%)
    ppermute x4, starting transfers between devices, swapped(): lax.ppermute(value, axis, [(i, i ^ apart) for i in range(lax.axis_size(ax...  7.68 us
    ppermute x4, waiting for transfers between devices, swapped(): lax.ppermute(value, axis, [(i, i ^ apart) for i in range(lax.axis_size(ax...  5.17 us
    pallas_call x1, Pallas kernels, kernel_and_sums(): pl.pallas_call(body, out_shape=(jax.ShapeDtypeStruct((rows, states), jnp....  2.34 us
    pallas_call x1, Pallas kernels, log_row_scaling(): pl.pallas_call(body, out_shape=jax.ShapeDtypeStruct((rows // LANES, LANES...  0.96 us
  transfers between devices with their start and end apart: 4, of which 4 were waited for; matrix products, arithmetic and copies ran while one was open for 0% of the time, Pallas kernels for 0%

profile of v2, /device:TPU:0, one launch (start us, length us, event | category | flops | bytes accessed | tf_op | source)
XLA Modules:
  0.0 16.2 jit_solution(11026023871410513389)
XLA Ops:
  0.0 0.0 copy-start
  0.0 0.0 copy-start.1
  0.0 2.3 %kernel_and_sums.1 = (f32[256,4096]{1,0:T(8,128)S(1)}, f32[32,128]{1,0:T(8,128)S(1)}) custom-call(f32[256,4096]{1,0:T(8,128)} %cost_ref.1), custom_call_target="tpu_custom_call" | custom-call | tf_op jit(solution)/shard_map/kernel_and_sums/pallas_call | solution.py:56
  2.4 0.6 %collective-permute-start = (f32[32,128]{1,0:T(8,128)S(1)}, f32[32,128]{1,0:T(8,128)S(1)}, u32[]{:S(2)}, u32[]{:S(2)}) collective-permute-start(f32[32,128]{1,0:T(8,128)S(1)} %get-tuple-element.8), channel_id=1, source_target_pairs={{0,1},{1,0},{2,3},{3,2},{4,5},{5,4},{6,7},{7,6},{8,9},{9,8},{10,11... | collective-permute-start | bytes 49160 | tf_op jit(solution)/shard_map/ppermute | solution.py:19
  2.9 0.8 %collective-permute-done = f32[32,128]{1,0:T(8,128)S(1)} collective-permute-done((f32[32,128]{1,0:T(8,128)S(1)}, f32[32,128]{1,0:T(8,128)S(1)}, u32[]{:S(2)}, u32[]{:S(2)}) %collective-permute-start) | collective-permute-done | bytes 16416 | tf_op jit(solution)/shard_map/ppermute | solution.py:19
  3.8 2.6 %collective-permute-start.1 = (f32[32,128]{1,0:T(8,128)S(1)}, f32[32,128]{1,0:T(8,128)S(1)}, u32[]{:S(2)}, u32[]{:S(2)}) collective-permute-start(f32[32,128]{1,0:T(8,128)S(1)} %add.9), channel_id=1, source_target_pairs={{0,3},{1,2},{2,1},{3,0},{4,7},{5,6},{6,5},{7,4},{8,11},{9,10},{10,... | collective-permute-start | bytes 49160 | tf_op jit(solution)/shard_map/ppermute | solution.py:19
  6.4 1.4 %collective-permute-done.1 = f32[32,128]{1,0:T(8,128)S(1)} collective-permute-done((f32[32,128]{1,0:T(8,128)S(1)}, f32[32,128]{1,0:T(8,128)S(1)}, u32[]{:S(2)}, u32[]{:S(2)}) %collective-permute-start.1) | collective-permute-done | bytes 16416 | tf_op jit(solution)/shard_map/ppermute | solution.py:19
  7.8 1.8 %collective-permute-start.2 = (f32[32,128]{1,0:T(8,128)S(1)}, f32[32,128]{1,0:T(8,128)S(1)}, u32[]{:S(2)}, u32[]{:S(2)}) collective-permute-start(f32[32,128]{1,0:T(8,128)S(1)} %add.10), channel_id=1, source_target_pairs={{0,5},{1,4},{2,7},{3,6},{4,1},{5,0},{6,3},{7,2},{8,13},{9,12},{10,... | collective-permute-start | bytes 49160 | tf_op jit(solution)/shard_map/ppermute | solution.py:19
  9.6 1.4 %collective-permute-done.2 = f32[32,128]{1,0:T(8,128)S(1)} collective-permute-done((f32[32,128]{1,0:T(8,128)S(1)}, f32[32,128]{1,0:T(8,128)S(1)}, u32[]{:S(2)}, u32[]{:S(2)}) %collective-permute-start.2) | collective-permute-done | bytes 16416 | tf_op jit(solution)/shard_map/ppermute | solution.py:19
  11.0 2.7 %collective-permute-start.3 = (f32[32,128]{1,0:T(8,128)S(1)}, f32[32,128]{1,0:T(8,128)S(1)}, u32[]{:S(2)}, u32[]{:S(2)}) collective-permute-start(f32[32,128]{1,0:T(8,128)S(1)} %add.11.half_ref), channel_id=1, source_target_pairs={{0,9},{1,8},{2,11},{3,10},{4,13},{5,12},{6,15},{7,14},{8,1},{9,0},... | collective-permute-start | bytes 49160 | tf_op jit(solution)/shard_map/ppermute | solution.py:19
  13.8 1.4 %collective-permute-done.3.other_ref = f32[32,128]{1,0:T(8,128)S(1)} collective-permute-done((f32[32,128]{1,0:T(8,128)S(1)}, f32[32,128]{1,0:T(8,128)S(1)}, u32[]{:S(2)}, u32[]{:S(2)}) %collective-permute-start.3) | collective-permute-done | bytes 16416 | tf_op jit(solution)/shard_map/ppermute | solution.py:19
  15.2 0.0 copy-done
  15.2 0.0 copy-done.1
  15.2 1.0 %log_row_scaling.1 = f32[2,128]{1,0:T(2,128)} custom-call(f32[256,4096]{1,0:T(8,128)S(1)} %get-tuple-element.7.kernel_ref, f32[32,128]{1,0:T(8,128)S(1)} %add.11.half_ref, f32[32,128]{1,0:T(8,128)S(1)} %collective-permute-done.3.other_ref, f32[32,128]{1,0:T(8,128)S(1)} %bitcast.3, f32[2,128]{1,0:T(2,128)S(1)} %bitcast.4), custom_call_target="tpu_custom_call" | custom-call | tf_op jit(solution)/shard_map/log_row_scaling/pallas_call | solution.py:95
  (3 shorter events, 0.0 us)
Async XLA Ops:
  0.0 15.2 %copy-start = (f32[4096]{0:T(1024)S(1)}, f32[4096]{0:T(1024)}, u32[]{:S(2)}) copy-start(f32[4096]{0:T(1024)} %param.5) | copy-start | bytes 49156
  0.0 15.2 %copy-start.1 = (f32[256]{0:T(256)S(1)}, f32[256]{0:T(256)}, u32[]{:S(2)}) copy-start(f32[256]{0:T(256)} %param.4) | copy-start | bytes 3076
  2.4 1.4 %collective-permute-start = (f32[32,128]{1,0:T(8,128)S(1)}, f32[32,128]{1,0:T(8,128)S(1)}, u32[]{:S(2)}, u32[]{:S(2)}) collective-permute-start(f32[32,128]{1,0:T(8,128)S(1)} %get-tuple-element.8), channel_id=1, source_target_pairs={{0,1},{1,0},{2,3},{3,2},{4,5},{5,4},{6,7},{7,6},{8,9},{9,8},{10,11... | collective-permute-start | bytes 49160 | tf_op jit(solution)/shard_map/ppermute | solution.py:19
  3.8 4.1 %collective-permute-start.1 = (f32[32,128]{1,0:T(8,128)S(1)}, f32[32,128]{1,0:T(8,128)S(1)}, u32[]{:S(2)}, u32[]{:S(2)}) collective-permute-start(f32[32,128]{1,0:T(8,128)S(1)} %add.9), channel_id=1, source_target_pairs={{0,3},{1,2},{2,1},{3,0},{4,7},{5,6},{6,5},{7,4},{8,11},{9,10},{10,... | collective-permute-start | bytes 49160 | tf_op jit(solution)/shard_map/ppermute | solution.py:19
  7.8 3.2 %collective-permute-start.2 = (f32[32,128]{1,0:T(8,128)S(1)}, f32[32,128]{1,0:T(8,128)S(1)}, u32[]{:S(2)}, u32[]{:S(2)}) collective-permute-start(f32[32,128]{1,0:T(8,128)S(1)} %add.10), channel_id=1, source_target_pairs={{0,5},{1,4},{2,7},{3,6},{4,1},{5,0},{6,3},{7,2},{8,13},{9,12},{10,... | collective-permute-start | bytes 49160 | tf_op jit(solution)/shard_map/ppermute | solution.py:19
  11.0 4.2 %collective-permute-start.3 = (f32[32,128]{1,0:T(8,128)S(1)}, f32[32,128]{1,0:T(8,128)S(1)}, u32[]{:S(2)}, u32[]{:S(2)}) collective-permute-start(f32[32,128]{1,0:T(8,128)S(1)} %add.11.half_ref), channel_id=1, source_target_pairs={{0,9},{1,8},{2,11},{3,10},{4,13},{5,12},{6,15},{7,14},{8,1},{9,0},... | collective-permute-start | bytes 49160 | tf_op jit(solution)/shard_map/ppermute | solution.py:19

commit v3 on v2

--- a/solution.py
+++ b/solution.py
@@ -19,31 +19,57 @@
     return lax.ppermute(value, axis, [(i, i ^ apart) for i in range(lax.axis_size(axis))])
 
 
-def distances(width):
-    return [1 << bit_index | 1 for bit_index in range(width.bit_length() - 1)]
+def stages(width):
+    across = [1 << bit_index | 1 for bit_index in range(1, width.bit_length() - 1)]
+    if len(across) < 2:
+        return [[(apart, apart)] for apart in [*across, 1] if apart < width]
+    one, other, *rest = across
+    both = one ^ other | 1
+    last = [(both, both), (one, other), (other, one)]
+    return [*([(apart, apart)] for apart in rest), [(1, 1)], last]
+
+
+def exchanged(value, stage):
+    devices = range(lax.axis_size("chain"))
+    return [
+        lax.ppermute(value, "chain", [(i, i ^ (odd if i & 1 else even)) for i in devices])
+        for odd, even in stage
+    ]
 
 
 def butterfly_sum(vector, width):
-    for apart in distances(width):
-        vector = vector + swapped(vector, "chain", apart)
+    for stage in stages(width):
+        vector = sum(exchanged(vector, stage), vector)
     return vector
 
 
-def kernel_and_sums(cost):
+def kernel_and_sums(cost, final_marginal, marginals):
     rows, states = cost.shape
     tiles = states // LANES
     chunk = rows // CHUNKS
 
-    def body(cost_ref, kernel_ref, sums_ref, sems):
+    def body(cost_ref, final_ref, marginal_ref, kernel_ref, sums_ref, scaled_ref, target_ref, sems, small_sems):
         def copy(index):
             span = pl.ds(index * chunk, chunk)
             return pltpu.make_async_copy(cost_ref.at[span], kernel_ref.at[span], sems.at[index])
 
+        small = (
+            pltpu.make_async_copy(final_ref, scaled_ref, small_sems.at[0]),
+            pltpu.make_async_copy(marginal_ref, target_ref, small_sems.at[1]),
+        )
         for index in range(CHUNKS):
             copy(index).start()
+        for each in small:
+            each.start()
         totals = [jnp.zeros((SUBLANES, LANES), jnp.float32)] * tiles
         for index in range(CHUNKS):
             copy(index).wait()
+            if index == CHUNKS - 2:
+                for each in small:
+                    each.wait()
+                final = scaled_ref[...]
+                scaled_ref[...] = final * float(states)
+                target_ref[...] = target_ref[...] * jnp.sum(final, keepdims=True)
             for first in range(index * chunk, (index + 1) * chunk, SUBLANES):
                 for tile in range(tiles):
                     at = (pl.ds(first, SUBLANES), pl.ds(tile * LANES, LANES))
@@ -53,28 +79,27 @@
         for tile in range(tiles):
             sums_ref[pl.ds(tile, 1), :] = jnp.sum(totals[tile], axis=0, keepdims=True)
 
+    operands = (cost, final_marginal.reshape(tiles, LANES), marginals.reshape(rows // LANES, LANES))
+    shapes = ((rows, states), (tiles, LANES), (tiles, LANES), (rows // LANES, LANES))
     return pl.pallas_call(
         body,
-        out_shape=(
-            jax.ShapeDtypeStruct((rows, states), jnp.float32),
-            jax.ShapeDtypeStruct((tiles, LANES), jnp.float32),
-        ),
-        in_specs=[pl.BlockSpec(memory_space=pltpu.HBM)],
-        out_specs=[pl.BlockSpec(memory_space=pltpu.VMEM)] * 2,
-        scratch_shapes=[pltpu.SemaphoreType.DMA((CHUNKS,))],
+        out_shape=[jax.ShapeDtypeStruct(shape, jnp.float32) for shape in shapes],
+        in_specs=[pl.BlockSpec(memory_space=pltpu.HBM)] * 3,
+        out_specs=[pl.BlockSpec(memory_space=pltpu.VMEM)] * 4,
+        scratch_shapes=[pltpu.SemaphoreType.DMA((CHUNKS,)), pltpu.SemaphoreType.DMA((2,))],
         compiler_params=pltpu.CompilerParams(vmem_limit_bytes=16 << 20),
         name="kernel_and_sums",
-    )(pltpu.with_memory_space_constraint(cost, pltpu.HBM))
-
-
-def log_row_scaling(kernel, half, other_half, final_marginal, marginals):
+    )(*(pltpu.with_memory_space_constraint(operand, pltpu.HBM) for operand in operands))
+
+
+def log_row_scaling(kernel, parts, scaled, target):
     rows, states = kernel.shape
     tiles = states // LANES
 
-    def body(kernel_ref, half_ref, other_ref, final_ref, marginal_ref, out_ref, weight_ref):
-        final = final_ref[...]
-        weight_ref[...] = final * float(states) / (half_ref[...] + other_ref[...])
-        total = jnp.sum(final, keepdims=True)
+    def body(kernel_ref, scaled_ref, target_ref, *refs):
+        *part_refs, out_ref, weight_ref = refs
+        sums = sum((ref[...] for ref in part_refs[1:]), part_refs[0][...])
+        weight_ref[...] = scaled_ref[...] / sums
         weights = [
             jnp.broadcast_to(weight_ref[pl.ds(tile, 1), :], (SUBLANES, LANES)) for tile in range(tiles)
         ]
@@ -90,32 +115,26 @@
             square = jnp.concatenate(partial[block * 16 : block * 16 + 16], axis=0)
             row_sums = jnp.sum(square.T, axis=0, keepdims=True)
             at = (pl.ds(block, 1), slice(None))
-            out_ref[at] = jnp.log(marginal_ref[at] * total / row_sums)
+            out_ref[at] = jnp.log(target_ref[at] / row_sums)
 
     return pl.pallas_call(
         body,
         out_shape=jax.ShapeDtypeStruct((rows // LANES, LANES), jnp.float32),
-        in_specs=[pl.BlockSpec(memory_space=pltpu.VMEM)] * 5,
+        in_specs=[pl.BlockSpec(memory_space=pltpu.VMEM)] * (3 + len(parts)),
         out_specs=pl.BlockSpec(memory_space=pltpu.VMEM),
         scratch_shapes=[pltpu.VMEM((tiles, LANES), jnp.float32)],
         compiler_params=pltpu.CompilerParams(vmem_limit_bytes=16 << 20),
         name="log_row_scaling",
-    )(
-        kernel,
-        half,
-        other_half,
-        final_marginal.reshape(tiles, LANES),
-        marginals.reshape(rows // LANES, LANES),
-    ).reshape(rows)
+    )(kernel, scaled, target, *parts).reshape(rows)
 
 
 def one_kernel(cost, marginals, final_marginal):
     width = cost.shape[1] // cost.shape[0]
-    kernel, sums = kernel_and_sums(cost)
-    *early, last = distances(width)
-    for apart in early:
-        sums = sums + swapped(sums, "chain", apart)
-    return log_row_scaling(kernel, sums, swapped(sums, "chain", last), final_marginal, marginals)
+    kernel, sums, scaled, target = kernel_and_sums(cost, final_marginal, marginals)
+    *early, last = stages(width)
+    for stage in early:
+        sums = sum(exchanged(sums, stage), sums)
+    return log_row_scaling(kernel, [sums, *exchanged(sums, last)], scaled, target)
 
 
 def from_behind(block, axis, distance):

time: 16.3 us -> 15.8 us (0.969)
  waiting for transfers between devices: 5.17 us -> 3.76 us
  starting transfers between devices: 7.68 us -> 8.55 us
    ppermute x4 -> x5, waiting for transfers between devices: 5.17 us -> 3.76 us  [exchanged(): lax.ppermute(value, 'chain', [(i, i ^ (odd if i & 1 else even)) for i in...]
    ppermute x4 -> x5, starting transfers between devices: 7.68 us -> 8.55 us  [exchanged(): lax.ppermute(value, 'chain', [(i, i ^ (odd if i & 1 else even)) for i in...]
  transfers between devices with their start and end apart: 4 -> 5, of which waited for: 4 -> 4; matrix products, arithmetic and copies ran while one was open for 0% -> 0% of each run, Pallas kernels for 0% -> 0%
where the time goes in v3:
time: 15.8 us; the launch traced here: 15.6 us
  starting transfers between devices  8.55 us (54%)
  waiting for transfers between devices  3.76 us (24%)
  Pallas kernels  3.28 us (21%)
    ppermute x5, starting transfers between devices, exchanged(): lax.ppermute(value, 'chain', [(i, i ^ (odd if i & 1 else even)) for i in...  8.55 us
    ppermute x5, waiting for transfers between devices, exchanged(): lax.ppermute(value, 'chain', [(i, i ^ (odd if i & 1 else even)) for i in...  3.76 us
    pallas_call x1, Pallas kernels, kernel_and_sums(): pl.pallas_call(body, out_shape=[jax.ShapeDtypeStruct(shape, jnp.float32)...  2.35 us
    pallas_call x1, Pallas kernels, log_row_scaling(): pl.pallas_call(body, out_shape=jax.ShapeDtypeStruct((rows // LANES, LANES...  0.94 us
  transfers between devices with their start and end apart: 5, of which 4 were waited for; matrix products, arithmetic and copies ran while one was open for 0% of the time, Pallas kernels for 0%

profile of v3, /device:TPU:0, one launch (start us, length us, event | category | flops | bytes accessed | tf_op | source)
XLA Modules:
  0.0 15.6 jit_solution(10335046297685575332)
XLA Ops:
  0.0 2.3 %kernel_and_sums.1 = (f32[256,4096]{1,0:T(8,128)S(1)}, f32[32,128]{1,0:T(8,128)S(1)}, f32[32,128]{1,0:T(8,128)S(1)}, f32[2,128]{1,0:T(2,128)S(1)}) custom-call(f32[256,4096]{1,0:T(8,128)} %cost_ref.1, f32[32,128]{1,0:T(8,128)} %bitcast.3, f32[2,128]{1,0:T(2,128)} %bitcast.4), custom_call_target="tpu_custom_call" | custom-call | tf_op jit(solution)/shard_map/kernel_and_sums/pallas_call | solution.py:84
  2.4 3.6 %collective-permute-start = (f32[32,128]{1,0:T(8,128)S(1)}, f32[32,128]{1,0:T(8,128)S(1)}, u32[]{:S(2)}, u32[]{:S(2)}) collective-permute-start(f32[32,128]{1,0:T(8,128)S(1)} %get-tuple-element.12), channel_id=1, source_target_pairs={{0,9},{1,8},{2,11},{3,10},{4,13},{5,12},{6,15},{7,14},{8,1},{9,0},... | collective-permute-start | bytes 49160 | tf_op jit(solution)/shard_map/ppermute | solution.py:35
  5.9 1.4 %collective-permute-done = f32[32,128]{1,0:T(8,128)S(1)} collective-permute-done((f32[32,128]{1,0:T(8,128)S(1)}, f32[32,128]{1,0:T(8,128)S(1)}, u32[]{:S(2)}, u32[]{:S(2)}) %collective-permute-start) | collective-permute-done | bytes 16416 | tf_op jit(solution)/shard_map/ppermute | solution.py:35
  7.4 0.7 %collective-permute-start.1 = (f32[32,128]{1,0:T(8,128)S(1)}, f32[32,128]{1,0:T(8,128)S(1)}, u32[]{:S(2)}, u32[]{:S(2)}) collective-permute-start(f32[32,128]{1,0:T(8,128)S(1)} %add.6), channel_id=1, source_target_pairs={{0,1},{1,0},{2,3},{3,2},{4,5},{5,4},{6,7},{7,6},{8,9},{9,8},{10,11... | collective-permute-start | bytes 49160 | tf_op jit(solution)/shard_map/ppermute | solution.py:35
  8.0 0.8 %collective-permute-done.1 = f32[32,128]{1,0:T(8,128)S(1)} collective-permute-done((f32[32,128]{1,0:T(8,128)S(1)}, f32[32,128]{1,0:T(8,128)S(1)}, u32[]{:S(2)}, u32[]{:S(2)}) %collective-permute-start.1) | collective-permute-done | bytes 16416 | tf_op jit(solution)/shard_map/ppermute | solution.py:35
  8.9 1.6 %collective-permute-start.4 = (f32[32,128]{1,0:T(8,128)S(1)}, f32[32,128]{1,0:T(8,128)S(1)}, u32[]{:S(2)}, u32[]{:S(2)}) collective-permute-start(f32[32,128]{1,0:T(8,128)S(1)} %add.7.refs_0_), channel_id=1, source_target_pairs={{0,3},{1,4},{2,1},{3,6},{4,7},{5,0},{6,5},{7,2},{8,11},{9,12},{10,... | collective-permute-start | bytes 49160 | tf_op jit(solution)/shard_map/ppermute | solution.py:35
  10.4 0.2 %collective-permute-start.3 = (f32[32,128]{1,0:T(8,128)S(1)}, f32[32,128]{1,0:T(8,128)S(1)}, u32[]{:S(2)}, u32[]{:S(2)}) collective-permute-start(f32[32,128]{1,0:T(8,128)S(1)} %add.7.refs_0_), channel_id=1, source_target_pairs={{0,5},{1,2},{2,7},{3,0},{4,1},{5,6},{6,3},{7,4},{8,13},{9,10},{10,... | collective-permute-start | bytes 49160 | tf_op jit(solution)/shard_map/ppermute | solution.py:35
  10.6 2.6 %collective-permute-start.2 = (f32[32,128]{1,0:T(8,128)S(1)}, f32[32,128]{1,0:T(8,128)S(1)}, u32[]{:S(2)}, u32[]{:S(2)}) collective-permute-start(f32[32,128]{1,0:T(8,128)S(1)} %add.7.refs_0_), channel_id=1, source_target_pairs={{0,7},{1,6},{2,5},{3,4},{4,3},{5,2},{6,1},{7,0},{8,15},{9,14},{10,... | collective-permute-start | bytes 49160 | tf_op jit(solution)/shard_map/ppermute | solution.py:35
  13.2 0.0 collective-permute-done.4.refs_3_
  13.2 0.4 %collective-permute-done.3.refs_2_ = f32[32,128]{1,0:T(8,128)S(1)} collective-permute-done((f32[32,128]{1,0:T(8,128)S(1)}, f32[32,128]{1,0:T(8,128)S(1)}, u32[]{:S(2)}, u32[]{:S(2)}) %collective-permute-start.3) | collective-permute-done | bytes 16416 | tf_op jit(solution)/shard_map/ppermute | solution.py:35
  13.6 1.1 %collective-permute-done.2.refs_1_ = f32[32,128]{1,0:T(8,128)S(1)} collective-permute-done((f32[32,128]{1,0:T(8,128)S(1)}, f32[32,128]{1,0:T(8,128)S(1)}, u32[]{:S(2)}, u32[]{:S(2)}) %collective-permute-start.2) | collective-permute-done | bytes 16416 | tf_op jit(solution)/shard_map/ppermute | solution.py:35
  14.7 0.9 %log_row_scaling.1 = f32[2,128]{1,0:T(2,128)} custom-call(f32[256,4096]{1,0:T(8,128)S(1)} %get-tuple-element.9.kernel_ref, f32[32,128]{1,0:T(8,128)S(1)} %get-tuple-element.10.scaled_ref, f32[2,128]{1,0:T(2,128)S(1)} %get-tuple-element.11.target_ref, f32[32,128]{1,0:T(8,128)S(1)} %add.7.refs_0_, f32[32,128]{1,0:T(8,128)S(1)} %collective-permute-done.2.refs_1_, ...), custom_call_target="tpu_custom_call" | custom-call | tf_op jit(solution)/shard_map/log_row_scaling/pallas_call | solution.py:120
  (2 shorter events, 0.0 us)
Async XLA Ops:
  2.4 5.0 %collective-permute-start = (f32[32,128]{1,0:T(8,128)S(1)}, f32[32,128]{1,0:T(8,128)S(1)}, u32[]{:S(2)}, u32[]{:S(2)}) collective-permute-start(f32[32,128]{1,0:T(8,128)S(1)} %get-tuple-element.12), channel_id=1, source_target_pairs={{0,9},{1,8},{2,11},{3,10},{4,13},{5,12},{6,15},{7,14},{8,1},{9,0},... | collective-permute-start | bytes 49160 | tf_op jit(solution)/shard_map/ppermute | solution.py:35
  7.4 1.5 %collective-permute-start.1 = (f32[32,128]{1,0:T(8,128)S(1)}, f32[32,128]{1,0:T(8,128)S(1)}, u32[]{:S(2)}, u32[]{:S(2)}) collective-permute-start(f32[32,128]{1,0:T(8,128)S(1)} %add.6), channel_id=1, source_target_pairs={{0,1},{1,0},{2,3},{3,2},{4,5},{5,4},{6,7},{7,6},{8,9},{9,8},{10,11... | collective-permute-start | bytes 49160 | tf_op jit(solution)/shard_map/ppermute | solution.py:35
  8.9 4.3 %collective-permute-start.4 = (f32[32,128]{1,0:T(8,128)S(1)}, f32[32,128]{1,0:T(8,128)S(1)}, u32[]{:S(2)}, u32[]{:S(2)}) collective-permute-start(f32[32,128]{1,0:T(8,128)S(1)} %add.7.refs_0_), channel_id=1, source_target_pairs={{0,3},{1,4},{2,1},{3,6},{4,7},{5,0},{6,5},{7,2},{8,11},{9,12},{10,... | collective-permute-start | bytes 49160 | tf_op jit(solution)/shard_map/ppermute | solution.py:35
  10.4 3.2 %collective-permute-start.3 = (f32[32,128]{1,0:T(8,128)S(1)}, f32[32,128]{1,0:T(8,128)S(1)}, u32[]{:S(2)}, u32[]{:S(2)}) collective-permute-start(f32[32,128]{1,0:T(8,128)S(1)} %add.7.refs_0_), channel_id=1, source_target_pairs={{0,5},{1,2},{2,7},{3,0},{4,1},{5,6},{6,3},{7,4},{8,13},{9,10},{10,... | collective-permute-start | bytes 49160 | tf_op jit(solution)/shard_map/ppermute | solution.py:35
  10.6 4.1 %collective-permute-start.2 = (f32[32,128]{1,0:T(8,128)S(1)}, f32[32,128]{1,0:T(8,128)S(1)}, u32[]{:S(2)}, u32[]{:S(2)}) collective-permute-start(f32[32,128]{1,0:T(8,128)S(1)} %add.7.refs_0_), channel_id=1, source_target_pairs={{0,7},{1,6},{2,5},{3,4},{4,3},{5,2},{6,1},{7,0},{8,15},{9,14},{10,... | collective-permute-start | bytes 49160 | tf_op jit(solution)/shard_map/ppermute | solution.py:35

commit v4 on v3

--- a/solution.py
+++ b/solution.py
@@ -19,8 +19,12 @@
     return lax.ppermute(value, axis, [(i, i ^ apart) for i in range(lax.axis_size(axis))])
 
 
+def distances(width):
+    return [1 << bit_index | 1 for bit_index in range(1, width.bit_length() - 1)]
+
+
 def stages(width):
-    across = [1 << bit_index | 1 for bit_index in range(1, width.bit_length() - 1)]
+    across = distances(width)
     if len(across) < 2:
         return [[(apart, apart)] for apart in [*across, 1] if apart < width]
     one, other, *rest = across
@@ -128,13 +132,27 @@
     )(kernel, scaled, target, *parts).reshape(rows)
 
 
+def summed_parts(sums, width):
+    across = distances(width)
+    if len(across) < 2:
+        return [butterfly_sum(sums, width)]
+    one, other, *rest = across
+    both = one ^ other | 1
+    for apart in rest:
+        sums = sums + swapped(sums, "chain", apart)
+    of_other_core = swapped(sums, "chain", 1)
+    far = swapped(sums, "chain", both)
+    whole = sums + of_other_core
+    (near,) = exchanged(whole, [(one, other)])
+    (side,) = exchanged(whole, [(other, one)])
+    far_of_other_core = swapped(far, "chain", 1)
+    return [whole, near, side, far, far_of_other_core]
+
+
 def one_kernel(cost, marginals, final_marginal):
     width = cost.shape[1] // cost.shape[0]
     kernel, sums, scaled, target = kernel_and_sums(cost, final_marginal, marginals)
-    *early, last = stages(width)
-    for stage in early:
-        sums = sum(exchanged(sums, stage), sums)
-    return log_row_scaling(kernel, [sums, *exchanged(sums, last)], scaled, target)
+    return log_row_scaling(kernel, summed_parts(sums, width), scaled, target)
 
 
 def from_behind(block, axis, distance):
@@ -167,7 +185,7 @@
     kernel = jnp.exp(-cost / entropic)
     scaling = jnp.ones((row_count,), jnp.float32)
     last_scaling = jnp.ones((states,), jnp.float32)
-    for sweep_index in range(SWEEPS):
+    for _ in range(SWEEPS):
         current = scaling
         alpha_start = jnp.ones((states,), jnp.float32)
         forward_state = (jnp.ones((row_count,), jnp.float32), current, alpha_start)
@@ -213,7 +231,7 @@
                 arrived = from_behind(backward_weighted_full * factor, "chain", -width)
                 carried_full = jnp.where(group == target_step - 1, arrived, carried_full)
             backward_state = (backward_beta_block, carried_full)
-        alpha_block, carried_unused, alpha_last = forward_state
+        alpha_block, _, alpha_last = forward_state
         beta_block = backward_state[0]
         scaling = marginals / (alpha_block * beta_block)
         last_scaling = final_marginal / alpha_last

time: 15.8 us -> 18 us (1.14)
  waiting for transfers between devices: 3.76 us -> 5.48 us
  starting transfers between devices: 8.55 us -> 9.03 us
    ppermute x0 -> x4, starting transfers between devices: none -> 7.24 us  [swapped(): lax.ppermute(value, axis, [(i, i ^ apart) for i in range(lax.axis_size(ax...]
    ppermute x5 -> x2, starting transfers between devices: 8.55 us -> 1.79 us  [exchanged(): lax.ppermute(value, 'chain', [(i, i ^ (odd if i & 1 else even)) for i in...]
    ppermute x0 -> x4, waiting for transfers between devices: none -> 2.5 us  [swapped(): lax.ppermute(value, axis, [(i, i ^ apart) for i in range(lax.axis_size(ax...]
    ppermute x5 -> x2, waiting for transfers between devices: 3.76 us -> 2.98 us  [exchanged(): lax.ppermute(value, 'chain', [(i, i ^ (odd if i & 1 else even)) for i in...]
  transfers between devices with their start and end apart: 5 -> 6, of which waited for: 4 -> 4; matrix products, arithmetic and copies ran while one was open for 0% -> 0% of each run, Pallas kernels for 0% -> 0%
where the time goes in v4:
time: 18 us; the launch traced here: 17.8 us
  starting transfers between devices  9.03 us (50%)
  waiting for transfers between devices  5.48 us (30%)
  Pallas kernels  3.28 us (18%)
    ppermute x4, starting transfers between devices, swapped(): lax.ppermute(value, axis, [(i, i ^ apart) for i in range(lax.axis_size(ax...  7.24 us
    ppermute x2, waiting for transfers between devices, exchanged(): lax.ppermute(value, 'chain', [(i, i ^ (odd if i & 1 else even)) for i in...  2.98 us
    ppermute x4, waiting for transfers between devices, swapped(): lax.ppermute(value, axis, [(i, i ^ apart) for i in range(lax.axis_size(ax...  2.5 us
    pallas_call x1, Pallas kernels, kernel_and_sums(): pl.pallas_call(body, out_shape=[jax.ShapeDtypeStruct(shape, jnp.float32)...  2.35 us
    ppermute x2, starting transfers between devices, exchanged(): lax.ppermute(value, 'chain', [(i, i ^ (odd if i & 1 else even)) for i in...  1.79 us
    pallas_call x1, Pallas kernels, log_row_scaling(): pl.pallas_call(body, out_shape=jax.ShapeDtypeStruct((rows // LANES, LANES...  0.94 us
  transfers between devices with their start and end apart: 6, of which 4 were waited for; matrix products, arithmetic and copies ran while one was open for 0% of the time, Pallas kernels for 0%

profile of v4, /device:TPU:0, one launch (start us, length us, event | category | flops | bytes accessed | tf_op | source)
XLA Modules:
  0.0 17.8 jit_solution(6180616385673732198)
XLA Ops:
  0.0 2.3 %kernel_and_sums.1 = (f32[256,4096]{1,0:T(8,128)S(1)}, f32[32,128]{1,0:T(8,128)S(1)}, f32[32,128]{1,0:T(8,128)S(1)}, f32[2,128]{1,0:T(2,128)S(1)}) custom-call(f32[256,4096]{1,0:T(8,128)} %cost_ref.1, f32[32,128]{1,0:T(8,128)} %bitcast.3, f32[2,128]{1,0:T(2,128)} %bitcast.4), custom_call_target="tpu_custom_call" | custom-call | tf_op jit(solution)/shard_map/kernel_and_sums/pallas_call | solution.py:88
  2.4 3.6 %collective-permute-start = (f32[32,128]{1,0:T(8,128)S(1)}, f32[32,128]{1,0:T(8,128)S(1)}, u32[]{:S(2)}, u32[]{:S(2)}) collective-permute-start(f32[32,128]{1,0:T(8,128)S(1)} %get-tuple-element.12), channel_id=1, source_target_pairs={{0,9},{1,8},{2,11},{3,10},{4,13},{5,12},{6,15},{7,14},{8,1},{9,0},... | collective-permute-start | bytes 49160 | tf_op jit(solution)/shard_map/ppermute | solution.py:19
  5.9 1.4 %collective-permute-done = f32[32,128]{1,0:T(8,128)S(1)} collective-permute-done((f32[32,128]{1,0:T(8,128)S(1)}, f32[32,128]{1,0:T(8,128)S(1)}, u32[]{:S(2)}, u32[]{:S(2)}) %collective-permute-start) | collective-permute-done | bytes 16416 | tf_op jit(solution)/shard_map/ppermute | solution.py:19
  7.4 2.8 %collective-permute-start.4 = (f32[32,128]{1,0:T(8,128)S(1)}, f32[32,128]{1,0:T(8,128)S(1)}, u32[]{:S(2)}, u32[]{:S(2)}) collective-permute-start(f32[32,128]{1,0:T(8,128)S(1)} %add.6), channel_id=1, source_target_pairs={{0,7},{1,6},{2,5},{3,4},{4,3},{5,2},{6,1},{7,0},{8,15},{9,14},{10,... | collective-permute-start | bytes 49160 | tf_op jit(solution)/shard_map/ppermute | solution.py:19
  10.2 0.4 %collective-permute-start.1 = (f32[32,128]{1,0:T(8,128)S(1)}, f32[32,128]{1,0:T(8,128)S(1)}, u32[]{:S(2)}, u32[]{:S(2)}) collective-permute-start(f32[32,128]{1,0:T(8,128)S(1)} %add.6), channel_id=1, source_target_pairs={{0,1},{1,0},{2,3},{3,2},{4,5},{5,4},{6,7},{7,6},{8,9},{9,8},{10,11... | collective-permute-start | bytes 49160 | tf_op jit(solution)/shard_map/ppermute | solution.py:19
  10.6 1.0 %collective-permute-done.4.refs_3_ = f32[32,128]{1,0:T(8,128)S(1)} collective-permute-done((f32[32,128]{1,0:T(8,128)S(1)}, f32[32,128]{1,0:T(8,128)S(1)}, u32[]{:S(2)}, u32[]{:S(2)}) %collective-permute-start.4) | collective-permute-done | bytes 16416 | tf_op jit(solution)/shard_map/ppermute | solution.py:19
  11.7 0.4 %collective-permute-start.5 = (f32[32,128]{1,0:T(8,128)S(1)}, f32[32,128]{1,0:T(8,128)S(1)}, u32[]{:S(2)}, u32[]{:S(2)}) collective-permute-start(f32[32,128]{1,0:T(8,128)S(1)} %collective-permute-done.4.refs_3_), channel_id=1, source_target_pairs={{0,1},{1,0},{2,3},{3,2},{4,5},{5,4},{6,7},{7,6},{8,9},{9,8},{10,11... | collective-permute-start | bytes 49160 | tf_op jit(solution)/shard_map/ppermute | solution.py:19
  12.1 0.0 collective-permute-done.1
  12.1 1.6 %collective-permute-start.3 = (f32[32,128]{1,0:T(8,128)S(1)}, f32[32,128]{1,0:T(8,128)S(1)}, u32[]{:S(2)}, u32[]{:S(2)}) collective-permute-start(f32[32,128]{1,0:T(8,128)S(1)} %add.7.refs_0_), channel_id=1, source_target_pairs={{0,3},{1,4},{2,1},{3,6},{4,7},{5,0},{6,5},{7,2},{8,11},{9,12},{10,... | collective-permute-start | bytes 49160 | tf_op jit(solution)/shard_map/ppermute | solution.py:39
  13.7 0.2 collective-permute-start.2
  13.9 0.0 collective-permute-done.5.refs_4_
  13.9 1.4 %collective-permute-done.3.refs_2_ = f32[32,128]{1,0:T(8,128)S(1)} collective-permute-done((f32[32,128]{1,0:T(8,128)S(1)}, f32[32,128]{1,0:T(8,128)S(1)}, u32[]{:S(2)}, u32[]{:S(2)}) %collective-permute-start.3) | collective-permute-done | bytes 16416 | tf_op jit(solution)/shard_map/ppermute | solution.py:39
  15.3 1.6 %collective-permute-done.2.refs_1_ = f32[32,128]{1,0:T(8,128)S(1)} collective-permute-done((f32[32,128]{1,0:T(8,128)S(1)}, f32[32,128]{1,0:T(8,128)S(1)}, u32[]{:S(2)}, u32[]{:S(2)}) %collective-permute-start.2) | collective-permute-done | bytes 16416 | tf_op jit(solution)/shard_map/ppermute | solution.py:39
  16.9 0.9 %log_row_scaling.1 = f32[2,128]{1,0:T(2,128)} custom-call(f32[256,4096]{1,0:T(8,128)S(1)} %get-tuple-element.9.kernel_ref, f32[32,128]{1,0:T(8,128)S(1)} %get-tuple-element.10.scaled_ref, f32[2,128]{1,0:T(2,128)S(1)} %get-tuple-element.11.target_ref, f32[32,128]{1,0:T(8,128)S(1)} %add.7.refs_0_, f32[32,128]{1,0:T(8,128)S(1)} %collective-permute-done.2.refs_1_, ...), custom_call_target="tpu_custom_call" | custom-call | tf_op jit(solution)/shard_map/log_row_scaling/pallas_call | solution.py:124
  (2 shorter events, 0.0 us)
Async XLA Ops:
  2.4 5.0 %collective-permute-start = (f32[32,128]{1,0:T(8,128)S(1)}, f32[32,128]{1,0:T(8,128)S(1)}, u32[]{:S(2)}, u32[]{:S(2)}) collective-permute-start(f32[32,128]{1,0:T(8,128)S(1)} %get-tuple-element.12), channel_id=1, source_target_pairs={{0,9},{1,8},{2,11},{3,10},{4,13},{5,12},{6,15},{7,14},{8,1},{9,0},... | collective-permute-start | bytes 49160 | tf_op jit(solution)/shard_map/ppermute | solution.py:19
  7.4 4.3 %collective-permute-start.4 = (f32[32,128]{1,0:T(8,128)S(1)}, f32[32,128]{1,0:T(8,128)S(1)}, u32[]{:S(2)}, u32[]{:S(2)}) collective-permute-start(f32[32,128]{1,0:T(8,128)S(1)} %add.6), channel_id=1, source_target_pairs={{0,7},{1,6},{2,5},{3,4},{4,3},{5,2},{6,1},{7,0},{8,15},{9,14},{10,... | collective-permute-start | bytes 49160 | tf_op jit(solution)/shard_map/ppermute | solution.py:19
  10.2 1.9 %collective-permute-start.1 = (f32[32,128]{1,0:T(8,128)S(1)}, f32[32,128]{1,0:T(8,128)S(1)}, u32[]{:S(2)}, u32[]{:S(2)}) collective-permute-start(f32[32,128]{1,0:T(8,128)S(1)} %add.6), channel_id=1, source_target_pairs={{0,1},{1,0},{2,3},{3,2},{4,5},{5,4},{6,7},{7,6},{8,9},{9,8},{10,11... | collective-permute-start | bytes 49160 | tf_op jit(solution)/shard_map/ppermute | solution.py:19
  11.7 2.2 %collective-permute-start.5 = (f32[32,128]{1,0:T(8,128)S(1)}, f32[32,128]{1,0:T(8,128)S(1)}, u32[]{:S(2)}, u32[]{:S(2)}) collective-permute-start(f32[32,128]{1,0:T(8,128)S(1)} %collective-permute-done.4.refs_3_), channel_id=1, source_target_pairs={{0,1},{1,0},{2,3},{3,2},{4,5},{5,4},{6,7},{7,6},{8,9},{9,8},{10,11... | collective-permute-start | bytes 49160 | tf_op jit(solution)/shard_map/ppermute | solution.py:19
  12.1 3.2 %collective-permute-start.3 = (f32[32,128]{1,0:T(8,128)S(1)}, f32[32,128]{1,0:T(8,128)S(1)}, u32[]{:S(2)}, u32[]{:S(2)}) collective-permute-start(f32[32,128]{1,0:T(8,128)S(1)} %add.7.refs_0_), channel_id=1, source_target_pairs={{0,3},{1,4},{2,1},{3,6},{4,7},{5,0},{6,5},{7,2},{8,11},{9,12},{10,... | collective-permute-start | bytes 49160 | tf_op jit(solution)/shard_map/ppermute | solution.py:39
  13.7 3.2 %collective-permute-start.2 = (f32[32,128]{1,0:T(8,128)S(1)}, f32[32,128]{1,0:T(8,128)S(1)}, u32[]{:S(2)}, u32[]{:S(2)}) collective-permute-start(f32[32,128]{1,0:T(8,128)S(1)} %add.7.refs_0_), channel_id=1, source_target_pairs={{0,5},{1,2},{2,7},{3,0},{4,1},{5,6},{6,3},{7,4},{8,13},{9,10},{10,... | collective-permute-start | bytes 49160 | tf_op jit(solution)/shard_map/ppermute | solution.py:39

commit v5 on v4

--- a/solution.py
+++ b/solution.py
@@ -8,7 +8,7 @@
 SWEEPS = 2
 LANES = 128
 SUBLANES = 8
-CHUNKS = 8
+PARTS = (8, 8, 8, 4, 2, 2)
 
 
 entropic = 0.25
@@ -50,31 +50,31 @@
 def kernel_and_sums(cost, final_marginal, marginals):
     rows, states = cost.shape
     tiles = states // LANES
-    chunk = rows // CHUNKS
+    starts = [rows * sum(PARTS[:index]) // sum(PARTS) for index in range(len(PARTS) + 1)]
 
     def body(cost_ref, final_ref, marginal_ref, kernel_ref, sums_ref, scaled_ref, target_ref, sems, small_sems):
         def copy(index):
-            span = pl.ds(index * chunk, chunk)
+            span = pl.ds(starts[index], starts[index + 1] - starts[index])
             return pltpu.make_async_copy(cost_ref.at[span], kernel_ref.at[span], sems.at[index])
 
         small = (
             pltpu.make_async_copy(final_ref, scaled_ref, small_sems.at[0]),
             pltpu.make_async_copy(marginal_ref, target_ref, small_sems.at[1]),
         )
-        for index in range(CHUNKS):
+        for index in range(len(PARTS)):
             copy(index).start()
         for each in small:
             each.start()
         totals = [jnp.zeros((SUBLANES, LANES), jnp.float32)] * tiles
-        for index in range(CHUNKS):
+        for index in range(len(PARTS)):
             copy(index).wait()
-            if index == CHUNKS - 2:
+            if index == len(PARTS) - 2:
                 for each in small:
                     each.wait()
                 final = scaled_ref[...]
                 scaled_ref[...] = final * float(states)
                 target_ref[...] = target_ref[...] * jnp.sum(final, keepdims=True)
-            for first in range(index * chunk, (index + 1) * chunk, SUBLANES):
+            for first in range(starts[index], starts[index + 1], SUBLANES):
                 for tile in range(tiles):
                     at = (pl.ds(first, SUBLANES), pl.ds(tile * LANES, LANES))
                     value = jnp.exp2(kernel_ref[at] * EXP2_SCALE)
@@ -90,7 +90,7 @@
         out_shape=[jax.ShapeDtypeStruct(shape, jnp.float32) for shape in shapes],
         in_specs=[pl.BlockSpec(memory_space=pltpu.HBM)] * 3,
         out_specs=[pl.BlockSpec(memory_space=pltpu.VMEM)] * 4,
-        scratch_shapes=[pltpu.SemaphoreType.DMA((CHUNKS,)), pltpu.SemaphoreType.DMA((2,))],
+        scratch_shapes=[pltpu.SemaphoreType.DMA((len(PARTS),)), pltpu.SemaphoreType.DMA((2,))],
         compiler_params=pltpu.CompilerParams(vmem_limit_bytes=16 << 20),
         name="kernel_and_sums",
     )(*(pltpu.with_memory_space_constraint(operand, pltpu.HBM) for operand in operands))

time: 18 us -> 18 us (level)
  no operation moved by 1% of the time
where the time goes in v5:
time: 18 us; the launch traced here: 17.8 us
  starting transfers between devices  9.03 us (50%)
  waiting for transfers between devices  5.48 us (30%)
  Pallas kernels  3.27 us (18%)
    ppermute x4, starting transfers between devices, swapped(): lax.ppermute(value, axis, [(i, i ^ apart) for i in range(lax.axis_size(ax...  7.24 us
    ppermute x2, waiting for transfers between devices, exchanged(): lax.ppermute(value, 'chain', [(i, i ^ (odd if i & 1 else even)) for i in...  2.98 us
    ppermute x4, waiting for transfers between devices, swapped(): lax.ppermute(value, axis, [(i, i ^ apart) for i in range(lax.axis_size(ax...  2.5 us
    pallas_call x1, Pallas kernels, kernel_and_sums(): pl.pallas_call(body, out_shape=[jax.ShapeDtypeStruct(shape, jnp.float32)...  2.33 us
    ppermute x2, starting transfers between devices, exchanged(): lax.ppermute(value, 'chain', [(i, i ^ (odd if i & 1 else even)) for i in...  1.79 us
    pallas_call x1, Pallas kernels, log_row_scaling(): pl.pallas_call(body, out_shape=jax.ShapeDtypeStruct((rows // LANES, LANES...  0.94 us
  transfers between devices with their start and end apart: 6, of which 4 were waited for; matrix products, arithmetic and copies ran while one was open for 0% of the time, Pallas kernels for 0%

profile of v5, /device:TPU:0, one launch (start us, length us, event | category | flops | bytes accessed | tf_op | source)
XLA Modules:
  0.0 17.8 jit_solution(665220879728381336)
XLA Ops:
  0.0 2.3 %kernel_and_sums.1 = (f32[256,4096]{1,0:T(8,128)S(1)}, f32[32,128]{1,0:T(8,128)S(1)}, f32[32,128]{1,0:T(8,128)S(1)}, f32[2,128]{1,0:T(2,128)S(1)}) custom-call(f32[256,4096]{1,0:T(8,128)} %cost_ref.1, f32[32,128]{1,0:T(8,128)} %bitcast.3, f32[2,128]{1,0:T(2,128)} %bitcast.4), custom_call_target="tpu_custom_call" | custom-call | tf_op jit(solution)/shard_map/kernel_and_sums/pallas_call | solution.py:88
  2.3 3.6 %collective-permute-start = (f32[32,128]{1,0:T(8,128)S(1)}, f32[32,128]{1,0:T(8,128)S(1)}, u32[]{:S(2)}, u32[]{:S(2)}) collective-permute-start(f32[32,128]{1,0:T(8,128)S(1)} %get-tuple-element.12), channel_id=1, source_target_pairs={{0,9},{1,8},{2,11},{3,10},{4,13},{5,12},{6,15},{7,14},{8,1},{9,0},... | collective-permute-start | bytes 49160 | tf_op jit(solution)/shard_map/ppermute | solution.py:19
  5.9 1.4 %collective-permute-done = f32[32,128]{1,0:T(8,128)S(1)} collective-permute-done((f32[32,128]{1,0:T(8,128)S(1)}, f32[32,128]{1,0:T(8,128)S(1)}, u32[]{:S(2)}, u32[]{:S(2)}) %collective-permute-start) | collective-permute-done | bytes 16416 | tf_op jit(solution)/shard_map/ppermute | solution.py:19
  7.4 2.8 %collective-permute-start.4 = (f32[32,128]{1,0:T(8,128)S(1)}, f32[32,128]{1,0:T(8,128)S(1)}, u32[]{:S(2)}, u32[]{:S(2)}) collective-permute-start(f32[32,128]{1,0:T(8,128)S(1)} %add.6), channel_id=1, source_target_pairs={{0,7},{1,6},{2,5},{3,4},{4,3},{5,2},{6,1},{7,0},{8,15},{9,14},{10,... | collective-permute-start | bytes 49160 | tf_op jit(solution)/shard_map/ppermute | solution.py:19
  10.2 0.4 %collective-permute-start.1 = (f32[32,128]{1,0:T(8,128)S(1)}, f32[32,128]{1,0:T(8,128)S(1)}, u32[]{:S(2)}, u32[]{:S(2)}) collective-permute-start(f32[32,128]{1,0:T(8,128)S(1)} %add.6), channel_id=1, source_target_pairs={{0,1},{1,0},{2,3},{3,2},{4,5},{5,4},{6,7},{7,6},{8,9},{9,8},{10,11... | collective-permute-start | bytes 49160 | tf_op jit(solution)/shard_map/ppermute | solution.py:19
  10.6 1.0 %collective-permute-done.4.refs_3_ = f32[32,128]{1,0:T(8,128)S(1)} collective-permute-done((f32[32,128]{1,0:T(8,128)S(1)}, f32[32,128]{1,0:T(8,128)S(1)}, u32[]{:S(2)}, u32[]{:S(2)}) %collective-permute-start.4) | collective-permute-done | bytes 16416 | tf_op jit(solution)/shard_map/ppermute | solution.py:19
  11.6 0.4 %collective-permute-start.5 = (f32[32,128]{1,0:T(8,128)S(1)}, f32[32,128]{1,0:T(8,128)S(1)}, u32[]{:S(2)}, u32[]{:S(2)}) collective-permute-start(f32[32,128]{1,0:T(8,128)S(1)} %collective-permute-done.4.refs_3_), channel_id=1, source_target_pairs={{0,1},{1,0},{2,3},{3,2},{4,5},{5,4},{6,7},{7,6},{8,9},{9,8},{10,11... | collective-permute-start | bytes 49160 | tf_op jit(solution)/shard_map/ppermute | solution.py:19
  12.1 0.0 collective-permute-done.1
  12.1 1.6 %collective-permute-start.3 = (f32[32,128]{1,0:T(8,128)S(1)}, f32[32,128]{1,0:T(8,128)S(1)}, u32[]{:S(2)}, u32[]{:S(2)}) collective-permute-start(f32[32,128]{1,0:T(8,128)S(1)} %add.7.refs_0_), channel_id=1, source_target_pairs={{0,3},{1,4},{2,1},{3,6},{4,7},{5,0},{6,5},{7,2},{8,11},{9,12},{10,... | collective-permute-start | bytes 49160 | tf_op jit(solution)/shard_map/ppermute | solution.py:39
  13.7 0.2 collective-permute-start.2
  13.9 0.0 collective-permute-done.5.refs_4_
  13.9 1.4 %collective-permute-done.3.refs_2_ = f32[32,128]{1,0:T(8,128)S(1)} collective-permute-done((f32[32,128]{1,0:T(8,128)S(1)}, f32[32,128]{1,0:T(8,128)S(1)}, u32[]{:S(2)}, u32[]{:S(2)}) %collective-permute-start.3) | collective-permute-done | bytes 16416 | tf_op jit(solution)/shard_map/ppermute | solution.py:39
  15.3 1.6 %collective-permute-done.2.refs_1_ = f32[32,128]{1,0:T(8,128)S(1)} collective-permute-done((f32[32,128]{1,0:T(8,128)S(1)}, f32[32,128]{1,0:T(8,128)S(1)}, u32[]{:S(2)}, u32[]{:S(2)}) %collective-permute-start.2) | collective-permute-done | bytes 16416 | tf_op jit(solution)/shard_map/ppermute | solution.py:39
  16.9 0.9 %log_row_scaling.1 = f32[2,128]{1,0:T(2,128)} custom-call(f32[256,4096]{1,0:T(8,128)S(1)} %get-tuple-element.9.kernel_ref, f32[32,128]{1,0:T(8,128)S(1)} %get-tuple-element.10.scaled_ref, f32[2,128]{1,0:T(2,128)S(1)} %get-tuple-element.11.target_ref, f32[32,128]{1,0:T(8,128)S(1)} %add.7.refs_0_, f32[32,128]{1,0:T(8,128)S(1)} %collective-permute-done.2.refs_1_, ...), custom_call_target="tpu_custom_call" | custom-call | tf_op jit(solution)/shard_map/log_row_scaling/pallas_call | solution.py:124
  (2 shorter events, 0.0 us)
Async XLA Ops:
  2.3 5.0 %collective-permute-start = (f32[32,128]{1,0:T(8,128)S(1)}, f32[32,128]{1,0:T(8,128)S(1)}, u32[]{:S(2)}, u32[]{:S(2)}) collective-permute-start(f32[32,128]{1,0:T(8,128)S(1)} %get-tuple-element.12), channel_id=1, source_target_pairs={{0,9},{1,8},{2,11},{3,10},{4,13},{5,12},{6,15},{7,14},{8,1},{9,0},... | collective-permute-start | bytes 49160 | tf_op jit(solution)/shard_map/ppermute | solution.py:19
  7.4 4.3 %collective-permute-start.4 = (f32[32,128]{1,0:T(8,128)S(1)}, f32[32,128]{1,0:T(8,128)S(1)}, u32[]{:S(2)}, u32[]{:S(2)}) collective-permute-start(f32[32,128]{1,0:T(8,128)S(1)} %add.6), channel_id=1, source_target_pairs={{0,7},{1,6},{2,5},{3,4},{4,3},{5,2},{6,1},{7,0},{8,15},{9,14},{10,... | collective-permute-start | bytes 49160 | tf_op jit(solution)/shard_map/ppermute | solution.py:19
  10.2 1.9 %collective-permute-start.1 = (f32[32,128]{1,0:T(8,128)S(1)}, f32[32,128]{1,0:T(8,128)S(1)}, u32[]{:S(2)}, u32[]{:S(2)}) collective-permute-start(f32[32,128]{1,0:T(8,128)S(1)} %add.6), channel_id=1, source_target_pairs={{0,1},{1,0},{2,3},{3,2},{4,5},{5,4},{6,7},{7,6},{8,9},{9,8},{10,11... | collective-permute-start | bytes 49160 | tf_op jit(solution)/shard_map/ppermute | solution.py:19
  11.6 2.2 %collective-permute-start.5 = (f32[32,128]{1,0:T(8,128)S(1)}, f32[32,128]{1,0:T(8,128)S(1)}, u32[]{:S(2)}, u32[]{:S(2)}) collective-permute-start(f32[32,128]{1,0:T(8,128)S(1)} %collective-permute-done.4.refs_3_), channel_id=1, source_target_pairs={{0,1},{1,0},{2,3},{3,2},{4,5},{5,4},{6,7},{7,6},{8,9},{9,8},{10,11... | collective-permute-start | bytes 49160 | tf_op jit(solution)/shard_map/ppermute | solution.py:19
  12.1 3.2 %collective-permute-start.3 = (f32[32,128]{1,0:T(8,128)S(1)}, f32[32,128]{1,0:T(8,128)S(1)}, u32[]{:S(2)}, u32[]{:S(2)}) collective-permute-start(f32[32,128]{1,0:T(8,128)S(1)} %add.7.refs_0_), channel_id=1, source_target_pairs={{0,3},{1,4},{2,1},{3,6},{4,7},{5,0},{6,5},{7,2},{8,11},{9,12},{10,... | collective-permute-start | bytes 49160 | tf_op jit(solution)/shard_map/ppermute | solution.py:39
  13.7 3.2 %collective-permute-start.2 = (f32[32,128]{1,0:T(8,128)S(1)}, f32[32,128]{1,0:T(8,128)S(1)}, u32[]{:S(2)}, u32[]{:S(2)}) collective-permute-start(f32[32,128]{1,0:T(8,128)S(1)} %add.7.refs_0_), channel_id=1, source_target_pairs={{0,5},{1,2},{2,7},{3,0},{4,1},{5,6},{6,3},{7,4},{8,13},{9,10},{10,... | collective-permute-start | bytes 49160 | tf_op jit(solution)/shard_map/ppermute | solution.py:39
